TPU v7x, 32 devices: a whole 2x2x4 slice. The times are simulated.
32 devices in a mesh: parts: 2 (over y), gz: 8 (over z, x), gy: 2 (over core).
Axes of the slice: x: 2, y: 2, z: 4, core: 2. Of those that a mesh axis runs over, the one named last changes fastest.
Arguments:
- direction: float32 [3, 16, 128, 128], P(None, ('parts', 'gz'), 'gy'), parts along dimension 1, may hold values from -6 to 6
- region: int32 [16, 128, 128], P(('parts', 'gz'), 'gy'), parts along dimension 0, may hold values from 0 to 3
- saturation: float32 [3], replicated, may hold values from 0.5 to 2
- kernel_main: float32 [6, 16, 256, 128], P(None, 'gz', 'gy'), may hold values from -6 to 6
- kernel_nyq: float32 [6, 16, 256], P(None, 'gz', 'gy'), may hold values from -6 to 6
Outputs:
- field: float32 [3, 16, 128, 128], P(None, ('parts', 'gz'), 'gy'), parts along dimension 1
There are 2 independent parts, one for each index of `parts`. A program takes and returns all parts, laid end to end along the dimension named above; an argument that names none is the same for every part. Nothing has to cross between parts.
Inputs may be any that keep to these rules, and one draw needn't show every extreme that they name: `region`: 0 marks an empty cell; other ids name materials.
All inputs are finite; a program needn't handle non-finite values.
Results may differ from a plain program's by a relative error of at most 0.00007.
Values sent between devices are 32-bit elements; how exact they have to be, the bound alone decides.
A program may use at most 64 MiB of HBM per device.

v0:
```python
import functools
import math

import jax
import jax.numpy as jnp
import numpy as np
from jax import lax
from jax.experimental import pallas as pl
from jax.experimental.pallas import tpu as pltpu
from jax.sharding import PartitionSpec as P

exchange_stiffness = 0.25
tensor_index = ((0, 3, 4), (3, 1, 5), (4, 5, 2))
highest = lax.Precision.HIGHEST


def with_halo(cells, sides, width):
    for axis, dim in sides:
        count = lax.axis_size(axis)
        ends = count - 1
        head = lax.slice_in_dim(cells, 0, width, axis=dim)
        tail = lax.slice_in_dim(cells, cells.shape[dim] - width, cells.shape[dim], axis=dim)
        cells = jnp.concatenate(
            [
                lax.ppermute(tail, axis, [(i, (i + 1) % count) for i in range(ends)]),
                cells,
                lax.ppermute(head, axis, [((i + 1) % count, i) for i in range(ends)]),
            ],
            axis=dim,
        )
    return cells


def phase(first, second, period):
    product = first[:, None] * second[None, :] % period
    angle = 2.0 * math.pi / period * product.astype(jnp.float32)
    return (jnp.cos(angle), jnp.sin(angle))


def slot_frequency(slot_index, bit_count):
    device = slot_index // 2
    reversed_bits = jnp.zeros_like(device)
    for b in range(bit_count):
        reversed_bits = reversed_bits + device // 2**b % 2 * 2 ** (bit_count - 1 - b)
    return 2 * reversed_bits + slot_index % 2


def row_transform(plane):
    columns = plane.shape[2]
    row_count = plane.shape[1]
    positions = jnp.arange(columns, dtype=jnp.int32)
    cosine, sine = phase(positions, positions, 2 * columns)
    table = jnp.concatenate([cosine, -sine], axis=1)
    flat = plane.reshape(3 * row_count, columns)
    both = jnp.dot(flat, table, precision=highest).reshape(3, row_count, 2, columns)
    signs = 1.0 - 2.0 * (positions % 2).astype(jnp.float32)
    nyquist = jnp.dot(flat, signs, precision=highest).reshape(3, row_count)
    return (both[:, :, 0], both[:, :, 1], nyquist)


def column_transform(real_rows, imag_rows, nyquist, cosine, sine):
    new_real = jnp.einsum("kr,crx->ckx", cosine, real_rows, precision=highest) + jnp.einsum(
        "kr,crx->ckx", sine, imag_rows, precision=highest
    )
    new_imag = jnp.einsum("kr,crx->ckx", cosine, imag_rows, precision=highest) - jnp.einsum(
        "kr,crx->ckx", sine, real_rows, precision=highest
    )
    nyq_real = jnp.einsum("kr,cr->ck", cosine, nyquist, precision=highest)
    nyq_imag = -jnp.einsum("kr,cr->ck", sine, nyquist, precision=highest)
    return (jnp.stack([new_real, new_imag], axis=1), jnp.stack([nyq_real, nyq_imag], axis=1))


def plane_transform(values, cosine, sine, direction_sign):
    real_part = values[:, 0]
    imag_part = values[:, 1]
    new_real = jnp.einsum(
        "pz,cz...->cp...", cosine, real_part, precision=highest
    ) - direction_sign * jnp.einsum("pz,cz...->cp...", sine, imag_part, precision=highest)
    new_imag = jnp.einsum(
        "pz,cz...->cp...", cosine, imag_part, precision=highest
    ) + direction_sign * jnp.einsum("pz,cz...->cp...", sine, real_part, precision=highest)
    return jnp.stack([new_real, new_imag], axis=1)


def apply_kernel(spectra, kernel):
    pieces = []
    for i in range(3):
        summed = kernel[tensor_index[i][0]] * spectra[0]
        for j in (1, 2):
            summed = summed + kernel[tensor_index[i][j]] * spectra[j]
        pieces.append(summed)
    return jnp.stack(pieces)


def local(direction, region, saturation, kernel_main, kernel_nyq):
    columns = direction.shape[3]
    own_rows = direction.shape[2]
    groups_y = lax.axis_size("gy")
    groups_z = lax.axis_size("gz")
    bit_count = groups_z.bit_length() - 1
    rows_total = own_rows * groups_y
    period_y = 2 * rows_total
    period_z = 2 * groups_z
    period_x = 2 * columns
    spec_rows = period_y // groups_y
    y_index = lax.axis_index("gy")
    magnetic = (region > 0).astype(jnp.float32)
    strength = jnp.zeros(region.shape, jnp.float32)
    for r in range(saturation.shape[0]):
        strength = strength + jnp.where(region == r + 1, saturation[r], 0.0)
    magnet_plane = (direction * strength[None])[:, 0]
    gathered = lax.all_gather(magnet_plane, "gy", axis=1, tiled=True)
    frequency = y_index * spec_rows + jnp.arange(spec_rows, dtype=jnp.int32)
    cosine, sine = phase(frequency, jnp.arange(rows_total, dtype=jnp.int32), period_y)
    real_rows, imag_rows, nyquist = row_transform(gathered)
    spec_main, spec_nyq = column_transform(real_rows, imag_rows, nyquist, cosine, sine)
    slot_freq = slot_frequency(jnp.arange(period_z, dtype=jnp.int32), bit_count)
    plane_ids = jnp.arange(groups_z, dtype=jnp.int32)
    sent_main, sent_nyq = (
        lax.all_to_all(spec_main[:, :, None], "gz", split_axis=3, concat_axis=2, tiled=True),
        lax.all_to_all(spec_nyq[:, :, None], "gz", split_axis=3, concat_axis=2, tiled=True),
    )
    cosine, sine = phase(slot_freq, plane_ids, period_z)
    done_main = plane_transform(sent_main, cosine, sine, -1.0)
    done_nyq = plane_transform(sent_nyq, cosine, sine, -1.0)
    full_main, full_nyq = (
        lax.all_to_all(done_main, "gz", split_axis=2, concat_axis=3, tiled=True),
        lax.all_to_all(done_nyq, "gz", split_axis=2, concat_axis=3, tiled=True),
    )
    field_main = apply_kernel(full_main, kernel_main)
    field_nyq = apply_kernel(full_nyq, kernel_nyq)
    out_main, out_nyq = (
        lax.all_to_all(field_main, "gz", split_axis=3, concat_axis=2, tiled=True),
        lax.all_to_all(field_nyq, "gz", split_axis=3, concat_axis=2, tiled=True),
    )
    cosine, sine = phase(plane_ids, slot_freq, period_z)
    back_main = plane_transform(out_main, cosine, sine, 1.0)
    back_nyq = plane_transform(out_nyq, cosine, sine, 1.0)
    plane_main, plane_nyq = (
        lax.all_to_all(back_main, "gz", split_axis=2, concat_axis=3, tiled=True),
        lax.all_to_all(back_nyq, "gz", split_axis=2, concat_axis=3, tiled=True),
    )
    plane_main = plane_main[:, :, 0]
    plane_nyq = plane_nyq[:, :, 0]
    frequency = y_index * spec_rows + jnp.arange(spec_rows, dtype=jnp.int32)
    cosine, sine = phase(jnp.arange(rows_total, dtype=jnp.int32), frequency, period_y)
    term_real = jnp.einsum("yk,ckx->cyx", cosine, plane_main[:, 0], precision=highest) - jnp.einsum(
        "yk,ckx->cyx", sine, plane_main[:, 1], precision=highest
    )
    term_imag = jnp.einsum("yk,ckx->cyx", cosine, plane_main[:, 1], precision=highest) + jnp.einsum(
        "yk,ckx->cyx", sine, plane_main[:, 0], precision=highest
    )
    nyq_real = jnp.einsum("yk,ck->cy", cosine, plane_nyq[:, 0], precision=highest) - jnp.einsum(
        "yk,ck->cy", sine, plane_nyq[:, 1], precision=highest
    )
    nyq_imag = jnp.einsum("yk,ck->cy", cosine, plane_nyq[:, 1], precision=highest) + jnp.einsum(
        "yk,ck->cy", sine, plane_nyq[:, 0], precision=highest
    )
    rows_main, rows_nyq = (
        lax.psum_scatter(
            jnp.stack([term_real, term_imag], axis=1), "gy", scatter_dimension=2, tiled=True
        ),
        lax.psum_scatter(
            jnp.stack([nyq_real, nyq_imag], axis=1), "gy", scatter_dimension=2, tiled=True
        ),
    )
    positions = jnp.arange(columns, dtype=jnp.int32)
    cosine, sine = phase(positions, positions, period_x)
    weights = jnp.where(positions == 0, 1.0, 2.0).astype(jnp.float32)[:, None]
    table = jnp.concatenate([weights * cosine, -weights * sine], axis=0)
    flat = jnp.concatenate([rows_main[:, 0], rows_main[:, 1]], axis=2).reshape(
        3 * own_rows, 2 * columns
    )
    signs = 1.0 - 2.0 * (positions % 2).astype(jnp.float32)
    demag = jnp.dot(flat, table, precision=highest).reshape(3, own_rows, columns)
    demag = demag + rows_nyq[:, 0][:, :, None] * signs[None, None, :]
    demag = demag * (1.0 / (period_x * period_y * period_z))
    moment = direction * magnetic[None]
    stacked = jnp.concatenate([moment, magnetic[None]], axis=0)
    rim = with_halo(stacked, (("gz", 1), ("gy", 2)), 1)
    centre = rim[:, 1:2, 1:-1]
    near = rim[:, 0:1, 1:-1] + rim[:, 2:3, 1:-1] + rim[:, 1:2, :-2] + rim[:, 1:2, 2:]
    padded_x = jnp.pad(centre, ((0, 0), (0, 0), (0, 0), (1, 1)))
    near = near + padded_x[..., :-2] + padded_x[..., 2:]
    exchange = exchange_stiffness * magnetic[None] * (near[:3] - near[3:4] * direction)
    return demag[:, None] + exchange


MESH = pl.DeviceIdType.MESH
most_unrolled_planes = 16


def halves(table):
    high = table.astype(np.float32).astype(jnp.bfloat16)
    low = (table - high.astype(np.float64)).astype(np.float32).astype(jnp.bfloat16)
    return np.stack([high, low])


@functools.lru_cache(maxsize=None)
def tables(columns, rows_total, groups_y, groups_z):
    x = np.arange(columns)
    ang = np.pi / columns * (np.outer(x, x) % (2 * columns))
    c, s = np.cos(ang), np.sin(ang)
    fwd = np.block([[c, -s], [s, c]])
    w = np.where(x == 0, 1.0, 2.0)[:, None]
    inv = np.block([[w * c, w * s], [-w * s, w * c]])
    tx = np.stack([halves(fwd), halves(inv)])
    spec = 2 * rows_total // groups_y
    y = np.arange(rows_total)
    ty = []
    for g in range(groups_y):
        ky = g * spec + np.arange(spec)
        ang = np.pi / rows_total * (np.outer(ky, y) % (2 * rows_total))
        c, s = np.cos(ang), np.sin(ang)
        f = np.block([[c, s], [-s, c]])
        ty.append(np.stack([halves(f), halves(f.T)]))
    ty = np.stack(ty)
    signs = 1.0 - 2.0 * (x % 2)
    gather = np.zeros((6 * columns, columns))
    spread = np.zeros((columns, 6 * columns))
    for b in range(6):
        gather[b * columns : (b + 1) * columns, b] = signs
        gather[b * columns : (b + 1) * columns, b + 6] = signs
        spread[b, b * columns : (b + 1) * columns] = signs
    pick = np.zeros((3, 12, columns))
    for d in range(3):
        for i in range(3):
            for k in range(2):
                pick[d, tensor_index[i][(i + d) % 3] * 2 + k, i * 2 + k] = 1.0
    bits = groups_z.bit_length() - 1
    coef = np.zeros((groups_z, 4 * groups_z))
    plane = np.arange(groups_z)
    for g in range(groups_z):
        rev = sum(((g >> b) & 1) << (bits - 1 - b) for b in range(bits))
        for k in range(2):
            ang = np.pi / groups_z * ((2 * rev + k) * plane % (2 * groups_z))
            coef[g, 2 * k :: 4] = np.cos(ang)
            coef[g, 2 * k + 1 :: 4] = -np.sin(ang)
    return (
        tx,
        ty,
        gather.astype(jnp.bfloat16),
        spread.astype(jnp.bfloat16),
        pick.astype(np.float32),
        coef.astype(np.float32),
    )


def split(value):
    high = value.astype(jnp.bfloat16)
    return high, (value - high.astype(jnp.float32)).astype(jnp.bfloat16)


def mm(a, b):
    return jnp.dot(a, b, preferred_element_type=jnp.float32)


def fused(
    coef,
    sat,
    direction_hbm,
    region_hbm,
    pick_hbm,
    knyq_hbm,
    kmain_hbm,
    tx_hbm,
    ty_hbm,
    gather_hbm,
    spread_hbm,
    out,
    direction,
    region,
    pick,
    knyq,
    mom,
    strength,
    near_strength,
    exch,
    kmain,
    tx,
    ty,
    gather,
    spread,
    zh,
    zl,
    rh,
    rl,
    gh,
    gl,
    afull,
    apeer,
    xsend,
    xrecv,
    upsend,
    uprecv,
    dnsend,
    dnrecv,
    local_sem,
    ag_send,
    ag_ici,
    ag_d2d,
    ag_psend,
    s_send,
    s_recv,
    a_send,
    a_recv,
    x_ssem,
    x_rsem,
    up_ssem,
    up_rsem,
    dn_ssem,
    dn_rsem,
):
    planes = mom.shape[0]
    line = planes // 2
    rows_total = mom.shape[2]
    columns = mom.shape[3]
    rows = direction.shape[2]
    g = lax.axis_index("gz")
    c = lax.axis_index("gy")
    o = g // 2
    xi = g % 2
    side = g + 1 - 2 * xi
    own = pl.ds(pl.multiple_of(c * rows, rows), rows)
    other = pl.ds(pl.multiple_of((1 - c) * rows, rows), rows)
    peer_id = {"gz": g, "gy": 1 - c}
    side_id = {"gz": side, "gy": c}
    up_id = {"gz": g + 2, "gy": c}
    dn_id = {"gz": g - 2, "gy": c}
    after_id = {"gz": g + 1, "gy": c}
    before_id = {"gz": g - 1, "gy": c}
    has_up = o < line - 1
    has_dn = o > 0
    has_after = g < planes - 1
    has_before = g > 0

    barrier = pltpu.get_barrier_semaphore()
    pl.semaphore_signal(barrier, inc=1, device_id=peer_id, device_id_type=MESH)
    pl.semaphore_signal(barrier, inc=1, device_id=side_id, device_id_type=MESH)
    for cond, where in ((has_up, up_id), (has_dn, dn_id), (has_after, after_id), (has_before, before_id)):

        @pl.when(cond)
        def _(where=where):
            pl.semaphore_signal(barrier, inc=1, device_id=where, device_id_type=MESH)

    first = [
        pltpu.make_async_copy(direction_hbm, direction, local_sem.at[5]),
        pltpu.make_async_copy(region_hbm, region, local_sem.at[6]),
    ]
    for copy in first:
        copy.start()
    loads = [
        pltpu.make_async_copy(kmain_hbm, kmain, local_sem.at[0]),
        pltpu.make_async_copy(tx_hbm, tx, local_sem.at[1]),
        pltpu.make_async_copy(ty_hbm.at[c], ty, local_sem.at[2]),
        pltpu.make_async_copy(gather_hbm, gather, local_sem.at[3]),
        pltpu.make_async_copy(spread_hbm, spread, local_sem.at[4]),
        pltpu.make_async_copy(pick_hbm, pick, local_sem.at[7]),
        pltpu.make_async_copy(knyq_hbm, knyq, local_sem.at[8]),
    ]
    for copy in first:
        copy.wait()
    for copy in loads:
        copy.start()

    reg = region[0]
    s = jnp.zeros(reg.shape, jnp.float32)
    for r in range(sat.shape[0]):
        s = s + jnp.where(reg == r + 1, sat[r], 0.0)
    strength[own, :] = s
    for j in range(3):
        mom[g, j, own, :] = direction[j, 0] * s

    friends = 2
    for cond in (has_up, has_dn, has_after, has_before):
        friends = friends + jnp.where(cond, 1, 0)
    pl.semaphore_wait(barrier, friends)

    def chunk_copy(p, j, way):
        where = (up_id, dn_id, side_id)[way]
        block = mom.at[p, j, own, :]
        return pltpu.make_async_remote_copy(
            src_ref=block,
            dst_ref=block,
            send_sem=ag_send.at[way, p, j],
            recv_sem=ag_ici.at[p, j],
            device_id=where,
            device_id_type=MESH,
        )

    def peer_all(half):
        block = mom.at[:, :, half, :]
        return pltpu.make_async_remote_copy(
            src_ref=block,
            dst_ref=block,
            send_sem=ag_psend.at[0],
            recv_sem=ag_d2d.at[0],
            device_id=peer_id,
            device_id_type=MESH,
        )

    def peer_copy(p, j):
        block = mom.at[p, j, own, :]
        return pltpu.make_async_remote_copy(
            src_ref=block,
            dst_ref=block,
            send_sem=ag_psend.at[0],
            recv_sem=ag_d2d.at[0],
            device_id=peer_id,
            device_id_type=MESH,
        )

    def when(cond, action):
        pl.when(cond)(action)

    for j in range(3):
        when(has_up, lambda: chunk_copy(g, j, 0).start())
        when(has_dn, lambda: chunk_copy(g, j, 1).start())
        chunk_copy(g, j, 2).start()

    def strength_copy(way):
        where = (peer_id, after_id, before_id)[way]
        if way == 0:
            dst = strength.at[own, :]
        else:
            dst = near_strength.at[way - 1]
        return pltpu.make_async_remote_copy(
            src_ref=strength.at[own, :],
            dst_ref=dst,
            send_sem=s_send.at[way],
            recv_sem=s_recv.at[way],
            device_id=where,
            device_id_type=MESH,
        )

    for j in range(3):
        peer_copy(g, j).start()

    for h in range(1, line + 1):
        for j in range(3):
            if h < line:

                @pl.when(o >= h)
                def _():
                    p = g - 2 * h
                    chunk_copy(p, j, 2).wait_recv()
                    when(has_up, lambda: chunk_copy(p, j, 0).start())
                    chunk_copy(p, j, 2).start()
                    peer_copy(p, j).start()

                @pl.when(o + h < line)
                def _():
                    p = g + 2 * h
                    chunk_copy(p, j, 2).wait_recv()
                    when(has_dn, lambda: chunk_copy(p, j, 1).start())
                    chunk_copy(p, j, 2).start()
                    peer_copy(p, j).start()

            def side_arrived(p):
                chunk_copy(p, j, 2).wait_recv()
                peer_copy(p, j).start()

            if h == 1:
                side_arrived(side)
            else:
                when(o >= h - 1, lambda: side_arrived(side - 2 * (h - 1)))
                when(o + h - 1 < line, lambda: side_arrived(side + 2 * (h - 1)))

    strength_copy(0).start()
    when(has_after, lambda: strength_copy(1).start())
    when(has_before, lambda: strength_copy(2).start())
    for copy in loads:
        copy.wait()
    peer_all(other).wait_recv()

    step = 32
    for j in range(3):
        for top in range(0, rows_total, step):
            accs = [None] * 4
            for p in range(planes):
                m = mom[p, j, top : top + step, :]
                for q in range(4):
                    term = m * coef[g, 4 * p + q]
                    accs[q] = term if accs[q] is None else accs[q] + term
            for q in range(4):
                hi, lo = split(accs[q])
                at = (2 * j + q // 2) * rows_total + top
                lanes = slice((q % 2) * columns, (q % 2 + 1) * columns)
                zh[at : at + step, lanes] = hi
                zl[at : at + step, lanes] = lo

    nyq = [None, None]
    for b in range(6):
        band = slice(b * rows_total, (b + 1) * rows_total)
        hi, lo = zh[band, :], zl[band, :]
        res = mm(hi, tx[0, 0]) + mm(hi, tx[0, 1]) + mm(lo, tx[0, 0])
        signs = gather[b * columns : (b + 1) * columns, :]
        for q in range(2):
            lanes = slice(q * columns, (q + 1) * columns)
            band_out = slice(q * rows_total, (q + 1) * rows_total)
            cols = slice(b * columns, (b + 1) * columns)
            rhi, rlo = split(res[:, lanes])
            rh[band_out, cols] = rhi
            rl[band_out, cols] = rlo
            n = mm(hi[:, lanes], signs) + mm(lo[:, lanes], signs)
            nyq[q] = n if nyq[q] is None else nyq[q] + n
    nyq_cols = slice(6 * columns, 7 * columns)
    for q in range(2):
        band_out = slice(q * rows_total, (q + 1) * rows_total)
        rhi, rlo = split(nyq[q])
        rh[band_out, nyq_cols] = rhi
        rl[band_out, nyq_cols] = rlo

    spec = kmain.shape[2]

    def column_pass(t, b):
        cols = slice(b * columns, (b + 1) * columns)
        hi, lo = (rh, rl) if t == 0 else (gh, gl)
        hi, lo = hi[:, cols], lo[:, cols]
        return mm(ty[t, 0], hi) + mm(ty[t, 1], hi) + mm(ty[t, 0], lo)

    for k in range(2):
        spectra = [column_pass(0, 2 * j + k) for j in range(3)]
        for i in range(3):
            cols = slice((2 * i + k) * columns, (2 * i + k + 1) * columns)
            for q in range(2):
                band = slice(q * spec, (q + 1) * spec)
                total = kmain[tensor_index[i][0], k] * spectra[0][band]
                for j in (1, 2):
                    total = total + kmain[tensor_index[i][j], k] * spectra[j][band]
                hi, lo = split(total)
                gh[band, cols] = hi
                gl[band, cols] = lo
    spectrum = column_pass(0, 6)
    factors = knyq[...].reshape(12, spec)
    totals = [None, None]
    for d in range(3):
        factor = lax.dot_general(
            factors, pick[d], (((0,), (0,)), ((), ())), precision=highest, preferred_element_type=jnp.float32
        )
        moved = spectrum if d == 0 else pltpu.roll(spectrum, columns - 2 * d, 1)
        for q in range(2):
            term = factor * moved[q * spec : (q + 1) * spec]
            totals[q] = term if totals[q] is None else totals[q] + term
    for q in range(2):
        hi, lo = split(totals[q])
        gh[q * spec : (q + 1) * spec, nyq_cols] = hi
        gl[q * spec : (q + 1) * spec, nyq_cols] = lo

    back = column_pass(1, 6)
    nyq_back = [split(back[:rows_total]), split(back[rows_total:])]

    def a_copy(j):
        return pltpu.make_async_remote_copy(
            src_ref=afull.at[j, :, other, :],
            dst_ref=apeer.at[j],
            send_sem=a_send.at[j],
            recv_sem=a_recv.at[j],
            device_id=peer_id,
            device_id_type=MESH,
        )

    for j in range(3):
        for k in range(2):
            b = 2 * j + k
            back = column_pass(1, b)
            parts = [split(back[:rows_total]), split(back[rows_total:])]
            hi = jnp.concatenate([parts[0][0], parts[1][0]], axis=1)
            lo = jnp.concatenate([parts[0][1], parts[1][1]], axis=1)
            res = mm(hi, tx[1, 0]) + mm(hi, tx[1, 1]) + mm(lo, tx[1, 0])
            signs = spread[:, b * columns : (b + 1) * columns]
            for q in range(2):
                extra = mm(nyq_back[q][0], signs) + mm(nyq_back[q][1], signs)
                afull[j, 2 * k + q] = res[:, q * columns : (q + 1) * columns] + extra
        a_copy(j).start()

    def contribution(p, j):
        total = None
        for q in range(4):
            term = apeer[j, q] * coef[g, 4 * p + q]
            total = term if total is None else total + term
        return total

    def rs_copy(d, j, way):
        src, dst, ssem, rsem, where = (
            (xsend, xrecv, x_ssem, x_rsem, side_id),
            (upsend, uprecv, up_ssem, up_rsem, up_id),
            (dnsend, dnrecv, dn_ssem, dn_rsem, dn_id),
        )[way]
        return pltpu.make_async_remote_copy(
            src_ref=src.at[d, j],
            dst_ref=dst.at[d, j],
            send_sem=ssem.at[d, j],
            recv_sem=rsem.at[d, j],
            device_id=where,
            device_id_type=MESH,
        )

    def side_send(d, j):
        xsend[d, j] = contribution(2 * d + 1 - xi, j)
        rs_copy(d, j, 0).start()

    for j in range(3):
        a_copy(j).wait_recv()
        for q in range(4):
            apeer[j, q] = apeer[j, q] + afull[j, q, own, :]
        when(o + line - 1 < line, lambda: side_send(o + line - 1, j))
        when(o - line + 1 >= 0, lambda: side_send(o - line + 1, j))
    for h in range(line - 2, -1, -1):
        for j in range(3):
            if h == 0:
                side_send(o, j)
            else:
                when(o + h < line, lambda: side_send(o + h, j))
                when(o - h >= 0, lambda: side_send(o - h, j))

    def exchange():
        strength_copy(0).wait_recv()
        for way, cond in ((1, has_before), (2, has_after)):

            @pl.when(cond)
            def _(way=way):
                strength_copy(way).wait_recv()

            @pl.when(jnp.logical_not(cond))
            def _(way=way):
                near_strength[way - 1] = jnp.zeros(near_strength.shape[1:], jnp.float32)

        full = strength[...]
        inverse = jnp.where(full > 0, 1.0 / jnp.where(full > 0, full, 1.0), 0.0)
        present = jnp.where(full > 0, 1.0, 0.0)
        row_id = lax.broadcasted_iota(jnp.int32, full.shape, 0)
        col_id = lax.broadcasted_iota(jnp.int32, full.shape, 1)

        def plane_near(v):
            total = jnp.where(row_id > 0, pltpu.roll(v, 1, 0), 0.0)
            total = total + jnp.where(row_id < rows_total - 1, pltpu.roll(v, rows_total - 1, 0), 0.0)
            total = total + jnp.where(col_id > 0, pltpu.roll(v, 1, 1), 0.0)
            return total + jnp.where(col_id < columns - 1, pltpu.roll(v, columns - 1, 1), 0.0)

        for j in range(3):
            exch[j] = plane_near(mom[g, j] * inverse)
        exch[3] = plane_near(present)
        adjacent = []
        for way in range(2):
            near_s = near_strength[way]
            there = near_s > 0
            adjacent.append(
                (jnp.where(there, 1.0 / jnp.where(there, near_s, 1.0), 0.0), jnp.where(there, 1.0, 0.0))
            )
        count = exch[3, own, :] + adjacent[0][1] + adjacent[1][1]
        mask = jnp.where(region[0] > 0, exchange_stiffness, 0.0)
        lower = jnp.maximum(g - 1, 0)
        upper = jnp.minimum(g + 1, planes - 1)
        for j in range(3):
            near = exch[j, own, :] + mom[lower, j, own, :] * adjacent[0][0]
            near = near + mom[upper, j, own, :] * adjacent[1][0]
            out[j, 0] = mask * (near - count * direction[j, 0])

    for h in range(line - 1, 0, -1):
        for j in range(3):

            def hop(d, way, cond):
                stage, arrived = ((upsend, uprecv), (dnsend, dnrecv))[way - 1]
                rs_copy(d, j, 0).wait_recv()
                stage[d, j] = contribution(2 * d + xi, j) + xrecv[d, j]

                @pl.when(cond)
                def _():
                    rs_copy(d, j, way).wait_recv()
                    stage[d, j] = stage[d, j] + arrived[d, j]

                rs_copy(d, j, way).start()

            when(o + h < line, lambda: hop(o + h, 1, has_dn))
            when(o - h >= 0, lambda: hop(o - h, 2, has_up))
        if h == line - 1:
            exchange()

    scale = 1.0 / (4 * rows_total * columns * 2 * planes)
    for j in range(3):
        rs_copy(o, j, 0).wait_recv()
        exch[j, :rows, :] = contribution(g, j) + xrecv[o, j]

        @pl.when(has_dn)
        def _():
            rs_copy(o, j, 1).wait_recv()
            exch[j, :rows, :] = exch[j, :rows, :] + uprecv[o, j]

        @pl.when(has_up)
        def _():
            rs_copy(o, j, 2).wait_recv()
            exch[j, :rows, :] = exch[j, :rows, :] + dnrecv[o, j]

        out[j, 0] = out[j, 0] + exch[j, :rows, :] * scale

    peer_all(own).wait_send()
    strength_copy(0).wait_send()
    when(has_after, lambda: strength_copy(1).wait_send())
    when(has_before, lambda: strength_copy(2).wait_send())
    for j in range(3):
        a_copy(j).wait_send()
        for d in range(line):
            chunk_copy(2 * d + xi, j, 2).wait_send()
            rs_copy(d, j, 0).wait_send()

            @pl.when(jnp.logical_and(has_up, o >= d))
            def _():
                chunk_copy(2 * d + xi, j, 0).wait_send()

            @pl.when(jnp.logical_and(has_dn, o <= d))
            def _():
                chunk_copy(2 * d + xi, j, 1).wait_send()

            when(o < d, lambda: rs_copy(d, j, 1).wait_send())
            when(o > d, lambda: rs_copy(d, j, 2).wait_send())


def fused_local(direction, region, saturation, kernel_main, kernel_nyq):
    rows, columns = direction.shape[2:]
    planes = lax.axis_size("gz")
    groups_y = lax.axis_size("gy")
    rows_total = rows * groups_y
    spec = kernel_main.shape[2]
    line = planes // 2
    tx, ty, gather, spread, pick, coef = (
        jnp.asarray(t) for t in tables(columns, rows_total, groups_y, planes)
    )
    f32, bf16 = jnp.float32, jnp.bfloat16
    vmem = pl.BlockSpec(memory_space=pltpu.VMEM)
    smem = pl.BlockSpec(memory_space=pltpu.SMEM)
    hbm = pl.BlockSpec(memory_space=pltpu.HBM)
    dma = pltpu.SemaphoreType.DMA
    stage = pltpu.VMEM((line, 3, rows, columns), f32)
    return pl.pallas_call(
        fused,
        out_shape=jax.ShapeDtypeStruct(direction.shape, f32),
        in_specs=[smem, smem, hbm, hbm, hbm, hbm, hbm, hbm, hbm, hbm, hbm],
        out_specs=vmem,
        scratch_shapes=[
            pltpu.VMEM(direction.shape, f32),
            pltpu.VMEM(region.shape, jnp.int32),
            pltpu.VMEM(pick.shape, f32),
            pltpu.VMEM(kernel_nyq.shape, f32),
            pltpu.VMEM((planes, 3, rows_total, columns), f32),
            pltpu.VMEM((rows_total, columns), f32),
            pltpu.VMEM((2, rows, columns), f32),
            pltpu.VMEM((4, rows_total, columns), f32),
            pltpu.VMEM(kernel_main.shape, f32),
            pltpu.VMEM(tx.shape, bf16),
            pltpu.VMEM(ty.shape[1:], bf16),
            pltpu.VMEM(gather.shape, bf16),
            pltpu.VMEM(spread.shape, bf16),
            pltpu.VMEM((6 * rows_total, 2 * columns), bf16),
            pltpu.VMEM((6 * rows_total, 2 * columns), bf16),
            pltpu.VMEM((2 * rows_total, 7 * columns), bf16),
            pltpu.VMEM((2 * rows_total, 7 * columns), bf16),
            pltpu.VMEM((2 * spec, 7 * columns), bf16),
            pltpu.VMEM((2 * spec, 7 * columns), bf16),
            pltpu.VMEM((3, 4, rows_total, columns), f32),
            pltpu.VMEM((3, 4, rows, columns), f32),
            stage,
            stage,
            stage,
            stage,
            stage,
            stage,
            dma((9,)),
            dma((3, planes, 3)),
            dma((planes, 3)),
            dma((1,)),
            dma((1,)),
            dma((3,)),
            dma((3,)),
            dma((3,)),
            dma((3,)),
            dma((line, 3)),
            dma((line, 3)),
            dma((line, 3)),
            dma((line, 3)),
            dma((line, 3)),
            dma((line, 3)),
        ],
        compiler_params=pltpu.CompilerParams(
            collective_id=0, has_side_effects=True, vmem_limit_bytes=67043328
        ),
        name="field_kernel",
    )(coef, saturation, direction, region, pick, kernel_nyq, kernel_main, tx, ty, gather, spread)


def solution(mesh):
    placed = (
        P(None, ("parts", "gz"), "gy", None),
        P(("parts", "gz"), "gy", None),
        P(),
        P(None, "gz", "gy", None),
        P(None, "gz", "gy"),
    )
    small = mesh.shape["gz"] <= most_unrolled_planes and mesh.shape["gy"] == 2
    return jax.shard_map(
        fused_local if small else local,
        mesh=mesh,
        in_specs=placed,
        out_specs=P(None, ("parts", "gz"), "gy", None),
        check_vma=False,
    )
```

profile of v0, /device:TPU:0, one launch (start us, length us, event | category | flops | bytes accessed | tf_op | source)
XLA Modules:
  0.0 41.5 jit_solution(5778858102227799751)
XLA Ops:
  0.0 40.0 %field_kernel.1 = f32[3,1,64,128]{3,2,1,0:T(8,128)} custom-call(f32[8,32]{1,0:T(8,128)} %constant.17.clone.coef, f32[3]{0:T(128)} %sat.1, f32[3,1,64,128]{3,2,1,0:T(8,128)} %direction_hbm.1, s32[1,64,128]{2,1,0:T(8,128)} %region_hbm.1, f32[3,12,128]{2,1,0:T(8,128)} %constant.16.clone.pick_hbm, f32[6,2,128]{2,1,0:T(2,128)} %knyq_hbm.1, ...), custom_call_target="tpu_custom_call" | custom-call | tf_op jit(solution)/shard_map/field_kernel/pallas_call | solution.py:735
  40.0 1.5 %copy.13 = f32[3,1,64,128]{3,2,1,0:T(8,128)} copy(f32[3,1,64,128]{3,2,1,0:T(8,128)} %field_kernel.1) | data formatting | bytes 196608
where the time goes:
time: 41.7 us; the launch traced here: 41.5 us
  Pallas kernels  40 us (96%)
  local copies, waits for them, and re-layouts  1.54 us (4%)
    pallas_call x1, Pallas kernels, fused_local(): pl.pallas_call(fused, out_shape=jax.ShapeDtypeStruct(direction.shape, f32...  40 us
    unnamed x1, local copies, waits for them, and re-layouts  1.54 us

commit v1 on v0

v1 whole, which is shorter than its diff:
```python
import functools
import math

import jax
import jax.numpy as jnp
import numpy as np
from jax import lax
from jax.experimental import pallas as pl
from jax.experimental.pallas import tpu as pltpu
from jax.sharding import PartitionSpec as P

exchange_stiffness = 0.25
tensor_index = ((0, 3, 4), (3, 1, 5), (4, 5, 2))
highest = lax.Precision.HIGHEST


def with_halo(cells, sides, width):
    for axis, dim in sides:
        count = lax.axis_size(axis)
        ends = count - 1
        head = lax.slice_in_dim(cells, 0, width, axis=dim)
        tail = lax.slice_in_dim(cells, cells.shape[dim] - width, cells.shape[dim], axis=dim)
        cells = jnp.concatenate(
            [
                lax.ppermute(tail, axis, [(i, (i + 1) % count) for i in range(ends)]),
                cells,
                lax.ppermute(head, axis, [((i + 1) % count, i) for i in range(ends)]),
            ],
            axis=dim,
        )
    return cells


def phase(first, second, period):
    product = first[:, None] * second[None, :] % period
    angle = 2.0 * math.pi / period * product.astype(jnp.float32)
    return (jnp.cos(angle), jnp.sin(angle))


def slot_frequency(slot_index, bit_count):
    device = slot_index // 2
    reversed_bits = jnp.zeros_like(device)
    for b in range(bit_count):
        reversed_bits = reversed_bits + device // 2**b % 2 * 2 ** (bit_count - 1 - b)
    return 2 * reversed_bits + slot_index % 2


def row_transform(plane):
    columns = plane.shape[2]
    row_count = plane.shape[1]
    positions = jnp.arange(columns, dtype=jnp.int32)
    cosine, sine = phase(positions, positions, 2 * columns)
    table = jnp.concatenate([cosine, -sine], axis=1)
    flat = plane.reshape(3 * row_count, columns)
    both = jnp.dot(flat, table, precision=highest).reshape(3, row_count, 2, columns)
    signs = 1.0 - 2.0 * (positions % 2).astype(jnp.float32)
    nyquist = jnp.dot(flat, signs, precision=highest).reshape(3, row_count)
    return (both[:, :, 0], both[:, :, 1], nyquist)


def column_transform(real_rows, imag_rows, nyquist, cosine, sine):
    new_real = jnp.einsum("kr,crx->ckx", cosine, real_rows, precision=highest) + jnp.einsum(
        "kr,crx->ckx", sine, imag_rows, precision=highest
    )
    new_imag = jnp.einsum("kr,crx->ckx", cosine, imag_rows, precision=highest) - jnp.einsum(
        "kr,crx->ckx", sine, real_rows, precision=highest
    )
    nyq_real = jnp.einsum("kr,cr->ck", cosine, nyquist, precision=highest)
    nyq_imag = -jnp.einsum("kr,cr->ck", sine, nyquist, precision=highest)
    return (jnp.stack([new_real, new_imag], axis=1), jnp.stack([nyq_real, nyq_imag], axis=1))


def plane_transform(values, cosine, sine, direction_sign):
    real_part = values[:, 0]
    imag_part = values[:, 1]
    new_real = jnp.einsum(
        "pz,cz...->cp...", cosine, real_part, precision=highest
    ) - direction_sign * jnp.einsum("pz,cz...->cp...", sine, imag_part, precision=highest)
    new_imag = jnp.einsum(
        "pz,cz...->cp...", cosine, imag_part, precision=highest
    ) + direction_sign * jnp.einsum("pz,cz...->cp...", sine, real_part, precision=highest)
    return jnp.stack([new_real, new_imag], axis=1)


def apply_kernel(spectra, kernel):
    pieces = []
    for i in range(3):
        summed = kernel[tensor_index[i][0]] * spectra[0]
        for j in (1, 2):
            summed = summed + kernel[tensor_index[i][j]] * spectra[j]
        pieces.append(summed)
    return jnp.stack(pieces)


def local(direction, region, saturation, kernel_main, kernel_nyq):
    columns = direction.shape[3]
    own_rows = direction.shape[2]
    groups_y = lax.axis_size("gy")
    groups_z = lax.axis_size("gz")
    bit_count = groups_z.bit_length() - 1
    rows_total = own_rows * groups_y
    period_y = 2 * rows_total
    period_z = 2 * groups_z
    period_x = 2 * columns
    spec_rows = period_y // groups_y
    y_index = lax.axis_index("gy")
    magnetic = (region > 0).astype(jnp.float32)
    strength = jnp.zeros(region.shape, jnp.float32)
    for r in range(saturation.shape[0]):
        strength = strength + jnp.where(region == r + 1, saturation[r], 0.0)
    magnet_plane = (direction * strength[None])[:, 0]
    gathered = lax.all_gather(magnet_plane, "gy", axis=1, tiled=True)
    frequency = y_index * spec_rows + jnp.arange(spec_rows, dtype=jnp.int32)
    cosine, sine = phase(frequency, jnp.arange(rows_total, dtype=jnp.int32), period_y)
    real_rows, imag_rows, nyquist = row_transform(gathered)
    spec_main, spec_nyq = column_transform(real_rows, imag_rows, nyquist, cosine, sine)
    slot_freq = slot_frequency(jnp.arange(period_z, dtype=jnp.int32), bit_count)
    plane_ids = jnp.arange(groups_z, dtype=jnp.int32)
    sent_main, sent_nyq = (
        lax.all_to_all(spec_main[:, :, None], "gz", split_axis=3, concat_axis=2, tiled=True),
        lax.all_to_all(spec_nyq[:, :, None], "gz", split_axis=3, concat_axis=2, tiled=True),
    )
    cosine, sine = phase(slot_freq, plane_ids, period_z)
    done_main = plane_transform(sent_main, cosine, sine, -1.0)
    done_nyq = plane_transform(sent_nyq, cosine, sine, -1.0)
    full_main, full_nyq = (
        lax.all_to_all(done_main, "gz", split_axis=2, concat_axis=3, tiled=True),
        lax.all_to_all(done_nyq, "gz", split_axis=2, concat_axis=3, tiled=True),
    )
    field_main = apply_kernel(full_main, kernel_main)
    field_nyq = apply_kernel(full_nyq, kernel_nyq)
    out_main, out_nyq = (
        lax.all_to_all(field_main, "gz", split_axis=3, concat_axis=2, tiled=True),
        lax.all_to_all(field_nyq, "gz", split_axis=3, concat_axis=2, tiled=True),
    )
    cosine, sine = phase(plane_ids, slot_freq, period_z)
    back_main = plane_transform(out_main, cosine, sine, 1.0)
    back_nyq = plane_transform(out_nyq, cosine, sine, 1.0)
    plane_main, plane_nyq = (
        lax.all_to_all(back_main, "gz", split_axis=2, concat_axis=3, tiled=True),
        lax.all_to_all(back_nyq, "gz", split_axis=2, concat_axis=3, tiled=True),
    )
    plane_main = plane_main[:, :, 0]
    plane_nyq = plane_nyq[:, :, 0]
    frequency = y_index * spec_rows + jnp.arange(spec_rows, dtype=jnp.int32)
    cosine, sine = phase(jnp.arange(rows_total, dtype=jnp.int32), frequency, period_y)
    term_real = jnp.einsum("yk,ckx->cyx", cosine, plane_main[:, 0], precision=highest) - jnp.einsum(
        "yk,ckx->cyx", sine, plane_main[:, 1], precision=highest
    )
    term_imag = jnp.einsum("yk,ckx->cyx", cosine, plane_main[:, 1], precision=highest) + jnp.einsum(
        "yk,ckx->cyx", sine, plane_main[:, 0], precision=highest
    )
    nyq_real = jnp.einsum("yk,ck->cy", cosine, plane_nyq[:, 0], precision=highest) - jnp.einsum(
        "yk,ck->cy", sine, plane_nyq[:, 1], precision=highest
    )
    nyq_imag = jnp.einsum("yk,ck->cy", cosine, plane_nyq[:, 1], precision=highest) + jnp.einsum(
        "yk,ck->cy", sine, plane_nyq[:, 0], precision=highest
    )
    rows_main, rows_nyq = (
        lax.psum_scatter(
            jnp.stack([term_real, term_imag], axis=1), "gy", scatter_dimension=2, tiled=True
        ),
        lax.psum_scatter(
            jnp.stack([nyq_real, nyq_imag], axis=1), "gy", scatter_dimension=2, tiled=True
        ),
    )
    positions = jnp.arange(columns, dtype=jnp.int32)
    cosine, sine = phase(positions, positions, period_x)
    weights = jnp.where(positions == 0, 1.0, 2.0).astype(jnp.float32)[:, None]
    table = jnp.concatenate([weights * cosine, -weights * sine], axis=0)
    flat = jnp.concatenate([rows_main[:, 0], rows_main[:, 1]], axis=2).reshape(
        3 * own_rows, 2 * columns
    )
    signs = 1.0 - 2.0 * (positions % 2).astype(jnp.float32)
    demag = jnp.dot(flat, table, precision=highest).reshape(3, own_rows, columns)
    demag = demag + rows_nyq[:, 0][:, :, None] * signs[None, None, :]
    demag = demag * (1.0 / (period_x * period_y * period_z))
    moment = direction * magnetic[None]
    stacked = jnp.concatenate([moment, magnetic[None]], axis=0)
    rim = with_halo(stacked, (("gz", 1), ("gy", 2)), 1)
    centre = rim[:, 1:2, 1:-1]
    near = rim[:, 0:1, 1:-1] + rim[:, 2:3, 1:-1] + rim[:, 1:2, :-2] + rim[:, 1:2, 2:]
    padded_x = jnp.pad(centre, ((0, 0), (0, 0), (0, 0), (1, 1)))
    near = near + padded_x[..., :-2] + padded_x[..., 2:]
    exchange = exchange_stiffness * magnetic[None] * (near[:3] - near[3:4] * direction)
    return demag[:, None] + exchange


MESH = pl.DeviceIdType.MESH
line_chips = 4
scope = jax.named_scope


def halves(table):
    high = table.astype(np.float32).astype(jnp.bfloat16)
    low = (table - high.astype(np.float64)).astype(np.float32).astype(jnp.bfloat16)
    return np.stack([high, low])


@functools.lru_cache(maxsize=None)
def tables(columns, rows_total, groups_z):
    x = np.arange(columns)
    ang = np.pi / columns * (np.outer(x, x) % (2 * columns))
    c, s = np.cos(ang), np.sin(ang)
    fwd = np.block([[c, -s], [s, c]])
    w = np.where(x == 0, 1.0, 2.0)[:, None]
    inv = np.block([[w * c, w * s], [-w * s, w * c]])
    tx = np.stack([halves(fwd), halves(inv)])
    ky = np.arange(2 * rows_total)
    ang = np.pi / rows_total * (np.outer(ky, np.arange(rows_total)) % (2 * rows_total))
    c, s = np.cos(ang), np.sin(ang)
    f = np.block([[c, s], [-s, c]])
    scale = 1.0 / (4 * rows_total * columns * 2 * groups_z)
    pick = np.zeros((2, 3, 12, columns))
    for slot in range(2):
        for d in range(3):
            for i in range(3):
                pick[slot, d, tensor_index[i][(i + d) % 3] * 2 + slot, i] = 1.0
    bits = groups_z.bit_length() - 1
    coef = np.zeros((groups_z, 2, 1, max(columns, 4 * groups_z)))
    plane = np.arange(groups_z)
    for g in range(groups_z):
        rev = sum(((g >> b) & 1) << (bits - 1 - b) for b in range(bits))
        for core in range(2):
            for k in range(2):
                slot = (core + k) % 2
                ang = np.pi / groups_z * ((2 * rev + slot) * plane % (2 * groups_z))
                coef[g, core, 0, 2 * k : 4 * groups_z : 4] = np.cos(ang)
                coef[g, core, 0, 2 * k + 1 : 4 * groups_z : 4] = -np.sin(ang)
    return (
        tx,
        halves(f),
        halves(f.T * scale),
        pick.astype(np.float32),
        coef.astype(np.float32),
    )


def split(value):
    high = value.astype(jnp.bfloat16)
    return high, (value - high.astype(jnp.float32)).astype(jnp.bfloat16)


def mm(a, b):
    return jnp.dot(a, b, preferred_element_type=jnp.float32)


def mm3(a, b):
    return mm(a[0], b[0]) + mm(a[1], b[0]) + mm(a[0], b[1])


def when(cond, action):
    pl.when(cond)(action)


def fused(
    coef_hbm,
    sat_hbm,
    direction_hbm,
    region_hbm,
    pick_hbm,
    knyq_hbm,
    kmain_hbm,
    tx_hbm,
    tyf_hbm,
    tyi_hbm,
    out,
    coef,
    sat,
    direction,
    region,
    pick,
    knyq,
    nfac,
    mom,
    strength,
    near_strength,
    edge_out,
    edge_in,
    kfull,
    tx,
    tyf,
    tyi,
    zh,
    zl,
    xs,
    xr,
    nown,
    rh,
    rl,
    spectra,
    part,
    gh,
    gl,
    nback,
    afull,
    apeer,
    xsend,
    xrecv,
    zsend,
    zmid,
    zin,
    load_sem,
    side_ssem,
    side_rsem,
    zown_ssem,
    relay_ssem,
    z_rsem,
    s_ssem,
    s_rsem,
    e_ssem,
    e_rsem,
    k_ssem,
    k_rsem,
    xs_ssem,
    xs_rsem,
    a_ssem,
    a_rsem,
    rx_ssem,
    rx_rsem,
    rz_ssem,
    rm_rsem,
    rz_rsem,
):
    line = mom.shape[1]
    planes = 2 * line
    rows = mom.shape[3]
    columns = mom.shape[4]
    rows_total = 2 * rows
    spec = kmain_hbm.shape[2]
    freqs = 2 * spec
    g = lax.axis_index("gz")
    c = lax.axis_index("gy")
    o = g // 2
    xi = g % 2
    own = pl.ds(pl.multiple_of(c * rows, rows), rows)
    other = pl.ds(pl.multiple_of((1 - c) * rows, rows), rows)
    own_im = pl.ds(pl.multiple_of(rows_total + c * rows, rows), rows)
    other_im = pl.ds(pl.multiple_of(rows_total + (1 - c) * rows, rows), rows)
    own_freqs = pl.ds(pl.multiple_of(c * spec, spec), spec)
    peer_id = {"gz": g, "gy": 1 - c}
    side_id = {"gz": g + 1 - 2 * xi, "gy": c}

    def chip(steps):
        return {"gz": g + 2 * steps, "gy": c}

    has = {k: (o + k < line) if k > 0 else (o + k >= 0) for k in (1, -1, 2, -2, 3, -3)}
    after_id = {"gz": g + 1, "gy": c}
    before_id = {"gz": g - 1, "gy": c}
    has_after = g < planes - 1
    has_before = g > 0
    inner = jnp.logical_and(o > 0, o < line - 1)
    lower = o < line // 2

    barrier = pltpu.get_barrier_semaphore()
    friends = 2
    for where in (peer_id, side_id):
        pl.semaphore_signal(barrier, inc=1, device_id=where, device_id_type=MESH)
    for cond, where in [(has[k], chip(k)) for k in (1, -1, 2, -2)] + [(has_after, after_id), (has_before, before_id)]:
        friends = friends + jnp.where(cond, 1, 0)

        @pl.when(cond)
        def _(where=where):
            pl.semaphore_signal(barrier, inc=1, device_id=where, device_id_type=MESH)

    first = [
        pltpu.make_async_copy(region_hbm, region, load_sem.at[0]),
        pltpu.make_async_copy(sat_hbm, sat, load_sem.at[1]),
        pltpu.make_async_copy(direction_hbm, direction, load_sem.at[2]),
    ]
    for copy in first:
        copy.start()
    loads = [
        pltpu.make_async_copy(coef_hbm.at[g, c], coef, load_sem.at[3]),
        pltpu.make_async_copy(tx_hbm, tx, load_sem.at[4]),
        pltpu.make_async_copy(tyf_hbm, tyf, load_sem.at[5]),
        pltpu.make_async_copy(tyi_hbm, tyi, load_sem.at[6]),
        pltpu.make_async_copy(pick_hbm.at[c], pick, load_sem.at[7]),
        pltpu.make_async_copy(knyq_hbm, knyq.at[c], load_sem.at[8]),
        pltpu.make_async_copy(kmain_hbm.at[:, c], kfull.at[:, own_freqs, :], load_sem.at[9]),
    ]
    with scope("s01_load"):
        for copy in first:
            copy.wait()
    for copy in loads:
        copy.start()

    reg = region[0]
    s = jnp.zeros(reg.shape, jnp.float32)
    for r in range(sat_hbm.shape[0]):
        s = s + jnp.where(reg == r + 1, sat[r], 0.0)
    strength[...] = s
    for j in range(3):
        mom[xi, o, j] = direction[j, 0] * s
    brim = pl.ds(pl.multiple_of((1 - c) * (rows - 8), 8), 8)
    there = jnp.where(region[0, brim, :] > 0, 1.0, 0.0)
    for j in range(3):
        edge_out[j] = direction[j, 0, brim, :] * there
    edge_out[3] = there

    with scope("s02_barrier"):
        pl.semaphore_wait(barrier, friends)

    def remote(src, dst, ssem, rsem, where):
        return pltpu.make_async_remote_copy(
            src_ref=src, dst_ref=dst, send_sem=ssem, recv_sem=rsem, device_id=where, device_id_type=MESH
        )

    def z_copy(d, j, ssem, steps):
        block = mom.at[xi, d, j]
        return remote(block, block, ssem, z_rsem.at[d, j], chip(steps))

    def side_copy(d, j):
        block = mom.at[xi, d, j]
        return remote(block, block, side_ssem.at[0], side_rsem.at[j], side_id)

    ways = (1, -1, 2, -2)
    with scope("s03_send"):
        for j in range(3):
            for w, k in enumerate(ways):
                when(has[k], lambda: z_copy(o, j, zown_ssem.at[w], k).start())
            side_copy(o, j).start()
        edge = remote(edge_out, edge_in, e_ssem.at[0], e_rsem.at[0], peer_id)
        edge.start()
        swap_main = remote(
            kmain_hbm.at[:, 1 - c], kfull.at[:, own_freqs, :], k_ssem.at[0], k_rsem.at[0], peer_id
        )
        swap_main.start()
        swap_nyq = remote(knyq_hbm, knyq.at[c], k_ssem.at[1], k_rsem.at[1], peer_id)
        swap_nyq.start()

    def passing(k, j):
        d = o + k

        @pl.when(has[k])
        def _():
            z_copy(d, j, zown_ssem.at[0], -k).wait_recv()
            if k == 2:
                when(has[-1], lambda: z_copy(d, j, relay_ssem.at[1], -1).start())
            if k == -2:
                when(has[1], lambda: z_copy(d, j, relay_ssem.at[0], 1).start())
            side_copy(d, j).start()

    with scope("s04_ag"):
        for j in range(3):
            for k in (-1, 1, -2, 2):
                passing(k, j)
    with scope("s05_ag3"):
        for j in range(3):
            for k in (-3, 3):
                passing(k, j)

    def strength_copy(way):
        return remote(
            strength, near_strength.at[way], s_ssem.at[way], s_rsem.at[way], (after_id, before_id)[way]
        )

    when(has_after, lambda: strength_copy(0).start())
    when(has_before, lambda: strength_copy(1).start())
    with scope("s06_loads"):
        for copy in loads:
            copy.wait()
        swap_main.wait_recv()
        swap_nyq.wait_recv()

    lane = lax.broadcasted_iota(jnp.int32, (rows, columns), 1)
    signs = 1.0 - 2.0 * (lane % 2).astype(jnp.float32)
    signs_total = jnp.concatenate([signs, signs], axis=0)
    for h in range(2):
        factors = knyq[h].reshape(12, spec)
        for d in range(3):
            nfac[d, h * spec : (h + 1) * spec, :] = lax.dot_general(
                factors, pick[d], (((0,), (0,)), ((), ())), precision=highest, preferred_element_type=jnp.float32
            )

    def swap_copy(j):
        return remote(xs.at[j], xr.at[j], xs_ssem.at[0], xs_rsem.at[j], peer_id)

    def store_rows(target, re, im, block):
        lanes = slice(block * columns, (block + 1) * columns)
        for at, value in zip(target, (re, im), strict=True):
            hi, lo = split(value)
            rh[at, lanes] = hi
            rl[at, lanes] = lo

    step = 32
    for j in range(3):
        with scope("s07_wait%d" % j):
            remote(
                mom.at[1 - xi, :, j], mom.at[1 - xi, :, j], side_ssem.at[0], side_rsem.at[j], side_id
            ).wait_recv()
        with scope("s08_zx%d" % j):
            place = jnp.logical_or(lane[:step] == j, lane[:step] == j + 3)
            for top in range(0, rows, step):
                band = slice(top, top + step)
                accs = [None] * 4
                for p in range(planes):
                    m = mom[p % 2, p // 2, j, band, :]
                    for q in range(4):
                        term = m * coef[0, 4 * p + q]
                        accs[q] = term if accs[q] is None else accs[q] + term
                for q in range(4):
                    hi, lo = split(accs[q])
                    at = (q // 2) * rows + top
                    lanes = slice((q % 2) * columns, (q % 2 + 1) * columns)
                    zh[at : at + step, lanes] = hi
                    zl[at : at + step, lanes] = lo
                    total = jnp.sum(accs[q] * signs[:step], axis=1, keepdims=True)
                    if q < 2:
                        nown[q, band, :] = jnp.where(place, total, nown[q, band, :] if j > 0 else 0.0)
                    else:
                        xs[3, q - 2, band, :] = jnp.where(place, total, xs[3, q - 2, band, :] if j > 0 else 0.0)
            res = mm3((zh[...], zl[...]), (tx[0, 0], tx[0, 1]))
            for q in range(2):
                xs[j, q] = res[rows:, q * columns : (q + 1) * columns]
            swap_copy(j).start()
            if j == 2:
                swap_copy(3).start()
            store_rows((own, own_im), res[:rows, :columns], res[:rows, columns:], j)

    wide = 2 * columns

    def forward(pair):
        lanes = slice(pair * wide, (pair + 1) * wide)
        spectra[pair] = mm3((tyf[0], tyf[1]), (rh[:, lanes], rl[:, lanes]))

    def take(j):
        swap_copy(j).wait_recv()
        store_rows((other, other_im), xr[j, 0], xr[j, 1], j)

    blocks = [slice(b, b + 64) for b in range(0, freqs, 64)]
    with scope("s09_take01"):
        store_rows((own, own_im), nown[0], nown[1], 3)
        take(0)
        take(1)
    with scope("s10_y01"):
        forward(0)
        for i in range(3):
            for block in blocks:
                k0 = kfull[tensor_index[i][0], block, :]
                k1 = kfull[tensor_index[i][1], block, :]
                for q in range(2):
                    at = slice(q * freqs + block.start, q * freqs + block.stop)
                    part[i, at, :] = k0 * spectra[0, at, :columns] + k1 * spectra[0, at, columns:]
    with scope("s11_take23"):
        take(2)
        take(3)
    with scope("s12_y23"):
        forward(1)

    homes = (0, 2, 3)

    def multiply(i):
        lanes = slice(homes[i] * columns, (homes[i] + 1) * columns)
        for block in blocks:
            k2 = kfull[tensor_index[i][2], block, :]
            for q in range(2):
                at = slice(q * freqs + block.start, q * freqs + block.stop)
                hi, lo = split(part[i, at, :] + k2 * spectra[1, at, :columns])
                gh[at, lanes] = hi
                gl[at, lanes] = lo

    def backward(pair):
        lanes = slice(pair * wide, (pair + 1) * wide)
        return mm3((tyi[0], tyi[1]), (gh[:, lanes], gl[:, lanes]))

    def a_copy(j):
        return remote(afull.at[j, :, other, :], apeer.at[j], a_ssem.at[0], a_rsem.at[j], peer_id)

    def finish(i, re, im):
        re, im = split(re), split(im)
        both = [jnp.concatenate([re[h], im[h]], axis=1) for h in range(2)]
        res = mm3(both, (tx[1, 0], tx[1, 1]))
        for q in range(2):
            nyquist = nback[q * rows_total : (q + 1) * rows_total, i : i + 1]
            afull[i, q] = res[:, q * columns : (q + 1) * columns] + nyquist * signs_total
        a_copy(i).start()

    with scope("s13_apply0"):
        multiply(0)
        for q in range(2):
            at = slice(q * freqs, (q + 1) * freqs)
            spectrum = spectra[1, at, columns:]
            total = nfac[0] * spectrum
            for d in (1, 2):
                total = total + nfac[d] * pltpu.roll(spectrum, columns - d, 1)
            hi, lo = split(total)
            gh[at, columns:wide] = hi
            gl[at, columns:wide] = lo
    with scope("s14_inv0"):
        back = backward(0)
        nback[...] = back[:, columns:]
        finish(0, back[:rows_total, :columns], back[rows_total:, :columns])
    with scope("s15_inv12"):
        multiply(1)
        multiply(2)
        back = backward(1)
        for i in (1, 2):
            lanes = slice((i - 1) * columns, i * columns)
            finish(i, back[:rows_total, lanes], back[rows_total:, lanes])

    def contribution(p, j):
        total = None
        for q in range(4):
            a = afull[j, q, own, :] if q < 2 else apeer[j, q - 2]
            term = a * coef[0, 4 * p + q]
            total = term if total is None else total + term
        return total

    last = line - 1
    targets = [
        jnp.where(lower, last, 0),
        jnp.where(o == 0, 2, jnp.where(o == 1, 0, jnp.where(o == 2, last, 1))),
        jnp.where(o == 0, 1, jnp.where(o == last, 2, jnp.where(o == 1, 2, 1))),
        o,
    ]

    def rx_copy(d, j):
        return remote(xsend.at[d, j], xrecv.at[d, j], rx_ssem.at[0], rx_rsem.at[d, j], side_id)

    def side_send(d, j):
        xsend[d, j] = contribution(2 * d + 1 - xi, j)
        rx_copy(d, j).start()

    for j in range(3):
        with scope("s16_a%d" % j):
            a_copy(j).wait_recv()
        with scope("s17_xs%d" % j):
            side_send(targets[0], j)
    with scope("s18_xs"):
        for d in targets[1:]:
            for j in range(3):
                side_send(d, j)

    def exchange():
        edge.wait_recv()
        for way, cond in ((0, has_before), (1, has_after)):

            @pl.when(cond)
            def _(way=way):
                strength_copy(way).wait_recv()

            @pl.when(jnp.logical_not(cond))
            def _(way=way):
                near_strength[way] = jnp.zeros(near_strength.shape[1:], jnp.float32)

        present = jnp.where(region[0] > 0, 1.0, 0.0)
        row_id = lax.broadcasted_iota(jnp.int32, present.shape, 0)
        col_id = lax.broadcasted_iota(jnp.int32, present.shape, 1)

        def plane_near(v, j):
            above = jnp.where(c == 1, edge_in[j, 7:8, :], 0.0)
            below = jnp.where(c == 0, edge_in[j, 0:1, :], 0.0)
            total = jnp.where(row_id > 0, pltpu.roll(v, 1, 0), above)
            total = total + jnp.where(row_id < rows - 1, pltpu.roll(v, rows - 1, 0), below)
            total = total + jnp.where(col_id > 0, pltpu.roll(v, 1, 1), 0.0)
            return total + jnp.where(col_id < columns - 1, pltpu.roll(v, columns - 1, 1), 0.0)

        adjacent = []
        for way in range(2):
            near_s = near_strength[way]
            filled = near_s > 0
            adjacent.append(
                (jnp.where(filled, 1.0 / jnp.where(filled, near_s, 1.0), 0.0), jnp.where(filled, 1.0, 0.0))
            )
        count = plane_near(present, 3) + adjacent[0][1] + adjacent[1][1]
        mask = exchange_stiffness * present
        before = jnp.maximum(g - 1, 0)
        after = jnp.minimum(g + 1, planes - 1)
        for j in range(3):
            near = plane_near(direction[j, 0] * present, j)
            near = near + mom[before % 2, before // 2, j] * adjacent[0][0]
            near = near + mom[after % 2, after // 2, j] * adjacent[1][0]
            out[j, 0] = mask * (near - count * direction[j, 0])

    with scope("s19_exch"):
        exchange()

    def to_target(r, j, kind, steps):
        return remote(zsend.at[r, j], zin.at[kind, j], rz_ssem.at[0], rz_rsem.at[kind, j], chip(steps))

    def to_middle(j, steps):
        return remote(zsend.at[0, j], zmid.at[j], rz_ssem.at[0], rm_rsem.at[j], chip(steps))

    def merge(r, j):
        d = targets[r]
        rx_copy(d, j).wait_recv()
        zsend[r, j] = contribution(2 * d + xi, j) + xrecv[d, j]

    with scope("s20_far"):
        for j in range(3):
            merge(0, j)
            when(o == 0, lambda: to_middle(j, 1).start())
            when(o == last, lambda: to_middle(j, -1).start())
    with scope("s21_r1"):
        for j in range(3):
            merge(1, j)
            when(o == 0, lambda: to_target(1, j, 2, 2).start())
            when(o == last, lambda: to_target(1, j, 2, -2).start())
            when(o == 1, lambda: to_target(1, j, 1, -1).start())
            when(o == 2, lambda: to_target(1, j, 0, 1).start())
    with scope("s22_mid"):
        for j in range(3):

            @pl.when(inner)
            def _():
                to_middle(j, 1).wait_recv()
                zsend[0, j] = zsend[0, j] + zmid[j]
                when(o == 1, lambda: to_target(0, j, 2, 2).start())
                when(o == 2, lambda: to_target(0, j, 2, -2).start())

    with scope("s23_r2"):
        for j in range(3):
            merge(2, j)
            when(lower, lambda: to_target(2, j, 0, 1).start())
            when(jnp.logical_not(lower), lambda: to_target(2, j, 1, -1).start())
    with scope("s24_final"):
        for j in range(3):
            rx_copy(o, j).wait_recv()
            out[j, 0] = out[j, 0] + contribution(g, j) + xrecv[o, j]
        for j in range(3):
            for kind, cond in ((0, has[-1]), (1, has[1]), (2, None)):

                def add():
                    to_target(0, j, kind, 1).wait_recv()
                    out[j, 0] = out[j, 0] + zin[kind, j]

                if cond is None:
                    add()
                else:
                    when(cond, add)

    with scope("s25_drain"):
        remote(mom.at[xi], mom.at[xi], side_ssem.at[0], side_rsem.at[0], side_id).wait_send()
        three = mom.at[xi, 0]
        for w, k in enumerate(ways):
            when(has[k], lambda: remote(three, three, zown_ssem.at[w], z_rsem.at[0, 0], peer_id).wait_send())
        for w, cond in ((0, o == line - 2), (1, o == 1)):
            when(cond, lambda: remote(three, three, relay_ssem.at[w], z_rsem.at[0, 0], peer_id).wait_send())
        when(has_after, lambda: strength_copy(0).wait_send())
        when(has_before, lambda: strength_copy(1).wait_send())
        edge.wait_send()
        swap_main.wait_send()
        swap_nyq.wait_send()
        remote(xs, xr, xs_ssem.at[0], xs_rsem.at[0], peer_id).wait_send()
        remote(afull.at[:, :, other, :], apeer, a_ssem.at[0], a_rsem.at[0], peer_id).wait_send()
        remote(xsend, xrecv, rx_ssem.at[0], rx_rsem.at[0, 0], side_id).wait_send()
        remote(zsend, zin, rz_ssem.at[0], rz_rsem.at[0, 0], peer_id).wait_send()


def fused_local(direction, region, saturation, kernel_main, kernel_nyq):
    rows, columns = direction.shape[2:]
    planes = lax.axis_size("gz")
    rows_total = 2 * rows
    spec = kernel_main.shape[2]
    freqs = 2 * spec
    line = planes // 2
    tx, tyf, tyi, pick, coef = (jnp.asarray(t) for t in tables(columns, rows_total, planes))
    f32, bf16 = jnp.float32, jnp.bfloat16
    hbm = pl.BlockSpec(memory_space=pltpu.HBM)
    dma = pltpu.SemaphoreType.DMA

    def vmem(*shape, dtype=f32):
        return pltpu.VMEM(shape, dtype)

    operands = (coef, saturation, direction, region, pick, kernel_nyq, kernel_main, tx, tyf, tyi)
    return pl.pallas_call(
        fused,
        out_shape=pltpu.VMEM(direction.shape, f32),
        in_specs=[hbm] * len(operands),
        out_specs=pl.BlockSpec(memory_space=pltpu.VMEM),
        scratch_shapes=[
            pltpu.SMEM(coef.shape[2:], f32),
            pltpu.SMEM(saturation.shape, f32),
            vmem(*direction.shape),
            vmem(*region.shape, dtype=jnp.int32),
            vmem(*pick.shape[1:]),
            vmem(2, *kernel_nyq.shape),
            vmem(3, freqs, columns),
            vmem(2, line, 3, rows, columns),
            vmem(rows, columns),
            vmem(2, rows, columns),
            vmem(4, 8, columns),
            vmem(4, 8, columns),
            vmem(6, freqs, columns),
            vmem(*tx.shape, dtype=bf16),
            vmem(*tyf.shape, dtype=bf16),
            vmem(*tyi.shape, dtype=bf16),
            vmem(2 * rows, 2 * columns, dtype=bf16),
            vmem(2 * rows, 2 * columns, dtype=bf16),
            vmem(4, 2, rows, columns),
            vmem(4, 2, rows, columns),
            vmem(2, rows, columns),
            vmem(2 * rows_total, 4 * columns, dtype=bf16),
            vmem(2 * rows_total, 4 * columns, dtype=bf16),
            vmem(2, 2 * freqs, 2 * columns),
            vmem(3, 2 * freqs, columns),
            vmem(2 * freqs, 4 * columns, dtype=bf16),
            vmem(2 * freqs, 4 * columns, dtype=bf16),
            vmem(2 * rows_total, columns),
            vmem(3, 2, rows_total, columns),
            vmem(3, 2, rows, columns),
            vmem(line, 3, rows, columns),
            vmem(line, 3, rows, columns),
            vmem(3, 3, rows, columns),
            vmem(3, rows, columns),
            vmem(3, 3, rows, columns),
            dma((10,)),
            dma((1,)),
            dma((3,)),
            dma((4,)),
            dma((2,)),
            dma((line, 3)),
            dma((2,)),
            dma((2,)),
            dma((1,)),
            dma((1,)),
            dma((2,)),
            dma((2,)),
            dma((1,)),
            dma((4,)),
            dma((1,)),
            dma((3,)),
            dma((1,)),
            dma((line, 3)),
            dma((1,)),
            dma((3,)),
            dma((3, 3)),
        ],
        compiler_params=pltpu.CompilerParams(
            collective_id=0, has_side_effects=True, vmem_limit_bytes=32 * 1024 * 1024
        ),
        name="field_kernel",
    )(*(pltpu.with_memory_space_constraint(t, pltpu.HBM) for t in operands))


def solution(mesh):
    placed = (
        P(None, ("parts", "gz"), "gy", None),
        P(("parts", "gz"), "gy", None),
        P(),
        P(None, "gz", "gy", None),
        P(None, "gz", "gy"),
    )
    small = mesh.shape["gz"] == 2 * line_chips and mesh.shape["gy"] == 2
    return jax.shard_map(
        fused_local if small else local,
        mesh=mesh,
        in_specs=placed,
        out_specs=P(None, ("parts", "gz"), "gy", None),
        check_vma=False,
    )
```

time: 41.7 us -> 35.6 us (0.85)
  Pallas kernels: 40 us -> 34.8 us
  local copies, waits for them, and re-layouts: 1.54 us -> 0.64 us
    pallas_call x1, Pallas kernels: 40 us -> 34.8 us  [fused_local(): pl.pallas_call(fused, out_shape=pltpu.VMEM(direction.shape, f32), in_spec...]
    unnamed x1, local copies, waits for them, and re-layouts: 1.54 us -> 0.64 us
where the time goes in v1:
time: 35.6 us; the launch traced here: 35.4 us
  Pallas kernels  34.8 us (98%)
  local copies, waits for them, and re-layouts  0.64 us (2%)
    pallas_call x1, Pallas kernels, fused_local(): pl.pallas_call(fused, out_shape=pltpu.VMEM(direction.shape, f32), in_spec...  34.8 us

profile of v1, /device:TPU:0, one launch (start us, length us, event | category | flops | bytes accessed | tf_op | source)
XLA Modules:
  0.0 35.4 jit_solution(11601212650067777400)
XLA Ops:
  0.0 34.8 %field_kernel.1 = f32[3,1,64,128]{3,2,1,0:T(8,128)S(1)} custom-call(f32[8,2,1,128]{3,2,1,0:T(1,128)} %constant.14.clone.coef_hbm, f32[3]{0:T(128)} %sat_hbm.1, f32[3,1,64,128]{3,2,1,0:T(8,128)} %direction_hbm.1, s32[1,64,128]{2,1,0:T(8,128)} %region_hbm.1, f32[2,3,12,128]{3,2,1,0:T(8,128)} %constant.13.clone.pick_hbm, f32[6,2,128]{2,1,0:T(2,128)} %knyq_hbm.1, ...), custom_call_target="tpu_custom_call" | custom-call | tf_op jit(solution)/shard_map/field_kernel/pallas_call | solution.py:767
  34.8 0.6 %copy.12 = f32[3,1,64,128]{3,2,1,0:T(8,128)} copy(f32[3,1,64,128]{3,2,1,0:T(8,128)S(1)} %field_kernel.1) | data formatting | bytes 196608
